TPU v7x, 128 devices: a whole 4x4x4 slice. The times are simulated.
128 devices in a mesh: enc: 32 (over z, x, core), llm: 4 (over y).
Axes of the slice: x: 4, y: 4, z: 4, core: 2. Of those that a mesh axis runs over, the one named last changes fastest.
Arguments:
- patches: bfloat16 [16384, 5120], P('enc', 'llm'), may hold values from -6 to 6
- ln_gain: bfloat16 [1280], replicated, may hold values from 0.099609375 to 1.8984375
- w_in: bfloat16 [5120, 5120], P(None, 'llm'), may hold values from -0.078125 to 0.078125
- b_in: bfloat16 [5120], P('llm'), may hold values from -3 to 3
- w_out: bfloat16 [5120, 2048], P('llm'), may hold values from -0.078125 to 0.078125
- b_out: bfloat16 [2048], replicated, may hold values from -3 to 3
- owner: int32 [16384, 1], P(('enc', 'llm')), may hold values from 0 to 127; in each aligned block of 128 rows (0 to 127, 128 to 255, ...) at most 2 rows name the same one
- cotangent: bfloat16 [32768, 2048], P(('enc', 'llm')), may hold values from -6 to 6
Outputs:
- image_embeds: bfloat16 [32768, 2048], P(('enc', 'llm'))
- grad_w_in: float32 [5120, 5120], P('enc', 'llm')
- grad_w_out: float32 [5120, 2048], P('llm', 'enc')
- grad_patches: bfloat16 [16384, 5120], P('enc', 'llm')
Inputs may be any that keep to these rules, and one draw needn't show every extreme that they name: Among the 128 consecutive tokens of one aligned block, no owner is named more than 2 times, a bound that some block reaches.
All inputs are finite; a program needn't handle non-finite values.
Results may differ from a plain program's by a relative error of at most 0.018.
Values may be sent and summed in bfloat16 or wider, within the bound.
No kernel may reach another device: no remote copies, remote signals or barrier semaphores. Data moves between devices by JAX's collectives and lax.ppermute only.
A program may use at most 192 MiB of HBM per device.

v0:
```python
import jax
import jax.numpy as jnp
from jax import lax
from jax.experimental import pallas as pl
from jax.experimental.pallas import tpu as pltpu
from jax.sharding import Mesh
from jax.sharding import PartitionSpec as P


EPSILON = 1e-06
HALF_ROOT = 0.7071067811865476
DENSITY = 0.3989422804014327
RING = 4
BF = jnp.bfloat16
F32 = jnp.float32


def send(value, axis, reverse=False):
    pairs = []
    for place in range(RING):
        for core in range(2):
            to = (place + (1 - 2 * core) * (-1 if reverse else 1)) % RING
            if axis == "y":
                pairs.append((core * RING + place, core * RING + to))
            else:
                pairs.append((2 * place + core, 2 * to + core))
    return lax.ppermute(value, ("c", "y") if axis == "y" else (axis, "c"), pairs)


def send_across(value, axis):
    return lax.ppermute(value, axis, [(i, (i + 2) % RING) for i in range(RING)])


def swap(value):
    return lax.ppermute(value, "c", [(0, 1), (1, 0)])


def exchange(value, axis):
    return lax.all_to_all(value, axis, 0, 0, tiled=True)


def pick(stacked, index):
    return lax.dynamic_index_in_dim(stacked, index, 0, keepdims=False)


def t_dot(left, right):
    return lax.dot_general(left, right, (((0,), (0,)), ((), ())), preferred_element_type=F32)


def dot_t(left, right):
    return lax.dot_general(left, right, (((1,), (1,)), ((), ())), preferred_element_type=F32)


def plus(first, second):
    return first.astype(F32) + second.astype(F32)


def total(pieces):
    return jnp.sum(pieces.astype(F32), axis=0)


def weight_kernel(where, own_left, other_left, own_right, other_right, low, high, low_start, high_start):
    rows = low.shape[2]
    width = RING * rows

    def one(i, carry):
        cut = pl.ds(pl.multiple_of(i * width, width), width)
        own, other = (
            left[0, :, cut] if len(left.shape) == 3 else left[:, cut]
            for left in (own_left, other_left)
        )
        term = t_dot(own, own_right[...]) + t_dot(other, other_right[...])
        for x in range(2):
            start = 2 * rows * x
            low[2 * i + x, 0] = term[start : start + rows].astype(BF)
            high[0, 2 * i + x] = term[start + rows : start + 2 * rows].astype(BF)
        return carry

    lax.fori_loop(0, 2, one, 0)
    low_start[0] = low[where[0], 0]

    @pl.when(pl.program_id(0) == where[1])
    def _():
        high_start[...] = high[0]


def weight_terms(starts, own_left, other_left, own_right, other_right):
    tokens = own_left.shape[-2]
    columns = own_right.shape[1]
    if own_left.ndim == 3:
        width = own_left.shape[2]
        left = pl.BlockSpec((1, tokens, width), lambda z, where: (z, 0, 0))
    else:
        width = own_left.shape[1] // RING
        left = pl.BlockSpec((tokens, width), lambda z, where: (0, z))
    rows = width // (2 * RING)
    right = pl.BlockSpec((tokens, columns), lambda z, where: (0, 0))
    whole = jax.ShapeDtypeStruct((RING, RING, rows, columns), BF)
    first = jax.ShapeDtypeStruct((RING, rows, columns), BF)
    return pl.pallas_call(
        weight_kernel,
        grid_spec=pltpu.PrefetchScalarGridSpec(
            num_scalar_prefetch=1,
            grid=(RING,),
            in_specs=[left, left, right, right],
            out_specs=[
                pl.BlockSpec((RING, 1, rows, columns), lambda z, where: (0, z, 0, 0)),
                pl.BlockSpec((1, RING, rows, columns), lambda z, where: (z, 0, 0, 0)),
                pl.BlockSpec((1, rows, columns), lambda z, where: (z, 0, 0)),
                pl.BlockSpec((RING, rows, columns), lambda z, where: (0, 0, 0)),
            ],
        ),
        out_shape=[whole, whole, first, first],
        cost_estimate=cost(4 * RING * tokens * width * columns, 20_000_000),
    )(jnp.stack(starts), own_left, other_left, own_right, other_right)


def cost(flops, moved):
    return pl.CostEstimate(flops=flops, bytes_accessed=moved, transcendentals=0)


def hidden_kernel(where, part, weights, *refs):
    *earlier, out, filed = refs
    held = earlier[0]
    rows = part.shape[0] // 4

    def one(i, carry):
        cut = pl.ds(pl.multiple_of(i * rows, rows), rows)
        term = jnp.dot(part[cut], weights[0], preferred_element_type=F32)
        out[cut] = term + (held[...] if held.shape[0] == 1 else held[cut]).astype(F32)
        return carry

    lax.fori_loop(0, 4, one, 0)

    @pl.when(pl.program_id(0) == 0)
    def _():
        filed[0] = part[...]


def hidden_terms(block, part, weights, held, filed):
    tokens, width = part.shape
    units = weights.shape[2]
    cut = units // 2
    first = filed is None
    return pl.pallas_call(
        hidden_kernel,
        grid_spec=pltpu.PrefetchScalarGridSpec(
            num_scalar_prefetch=1,
            grid=(2,),
            in_specs=[
                pl.BlockSpec((tokens, width), lambda i, where: (0, 0)),
                pl.BlockSpec((1, width, cut), lambda i, where: (where[0], 0, i)),
                pl.BlockSpec((1 if first else tokens, cut), lambda i, where: (0, i)),
                *([] if first else [pl.BlockSpec(memory_space=pl.ANY)]),
            ],
            out_specs=[
                pl.BlockSpec((tokens, cut), lambda i, where: (0, i)),
                pl.BlockSpec((1, tokens, width), lambda i, where: (where[0], 0, 0)),
            ],
        ),
        out_shape=[
            jax.ShapeDtypeStruct((tokens, units), F32),
            jax.ShapeDtypeStruct((RING, tokens, width), BF),
        ],
        input_output_aliases={} if first else {4: 1},
        cost_estimate=cost(2 * tokens * width * units, 10_000_000),
    )(jnp.stack([block]), part, weights, held, *([] if first else [filed]))


def local(patches, ln_gain, w_in, b_in, w_out, b_out, owner, cotangent):
    z, x, core, y = (lax.axis_index(name) for name in ("z", "x", "c", "y"))
    way = 1 - 2 * core
    everyone = ("z", "x", "c", "y")
    devices = lax.axis_size(everyone)
    slot_cap = cotangent.shape[0] // devices
    tokens, width = patches.shape
    own_rows = tokens // RING
    gain = ln_gain.astype(F32)
    last = owner

    def send_all(in_pair, out_pair):
        low, high, out_low, out_high = lax.optimization_barrier((*in_pair, *out_pair))
        return (
            (send(low, "x"), send(high, "z")),
            (send(out_low, "x"), send(out_high, "z")),
        )

    def add_pair(terms, k, arrived):
        low = pick(terms[0], (x + way * k) % RING).astype(F32) + arrived[0].astype(F32)
        high = pick(terms[1], (z + way * k) % RING).astype(F32) + arrived[1].astype(F32)
        return low.astype(BF), high.astype(BF)

    def go(*values):
        out = lax.optimization_barrier((*values, last))[:-1]
        return out if len(out) > 1 else out[0]

    def mark(value):
        nonlocal last
        last = value
        return value

    def place(places):
        return (y + way * places) % RING

    targets = owner[:, 0]
    before = jnp.arange(own_rows)[:, None] > jnp.arange(own_rows)[None, :]
    same_owner = targets[:, None] == targets[None, :]
    rank_in = jnp.sum(jnp.logical_and(same_owner, before), axis=1)
    slot_ids = targets * slot_cap + rank_in
    placing = (
        jnp.arange(devices * slot_cap, dtype=jnp.int32)[:, None] == slot_ids[None, :]
    ).astype(BF)

    merged = patches.astype(F32)
    inverse = lax.rsqrt(jnp.mean(merged * merged, axis=-1, keepdims=True) + EPSILON)
    part = mark((merged * inverse * gain).astype(BF))
    coming = send(part, "y")
    returned = exchange(go(cotangent), everyone)

    w_in_blocks = w_in.reshape(RING, width, -1)
    hidden, normed = mark(
        hidden_terms(place(0), go(part), w_in_blocks, b_in[None], None)
    )
    part = go(coming)
    coming = send(part, "y")
    hidden, normed = mark(hidden_terms(place(-1), part, w_in_blocks, hidden, normed))
    part_grad = mark(t_dot(placing, go(returned)).astype(BF))
    coming_grad = send(part_grad, "y")
    grad_embeds = jnp.zeros((RING, *part_grad.shape), BF)
    grad_embeds = lax.dynamic_update_index_in_dim(grad_embeds, part_grad, y, 0)
    part = mark(go(coming))
    coming = send(part, "y")
    hidden, normed = mark(hidden_terms(place(-2), part, w_in_blocks, hidden, normed))
    part_grad = mark(go(coming_grad))
    coming_grad = send(part_grad, "y")
    grad_embeds = lax.dynamic_update_index_in_dim(grad_embeds, part_grad, place(-1), 0)
    part = mark(go(coming))
    normed = lax.dynamic_update_index_in_dim(normed, part, place(-3), 0)
    hidden = hidden + jnp.dot(
        part, pick(w_in_blocks, place(-3)), preferred_element_type=F32
    )
    other_normed = swap(normed)
    cdf = 0.5 * (1.0 + lax.erf(hidden * HALF_ROOT))
    active = mark((hidden * cdf).astype(BF))
    slope = cdf + hidden * jnp.exp(-0.5 * hidden * hidden) * DENSITY

    part_grad = mark(go(coming_grad))
    coming_grad = send(part_grad, "y")
    grad_embeds = lax.dynamic_update_index_in_dim(grad_embeds, part_grad, place(-2), 0)
    partial = jnp.dot(go(active), w_out, preferred_element_type=F32).astype(BF)
    mark(partial)
    pieces = exchange(partial.reshape(RING, own_rows, -1), "y")
    half = active.shape[1] // 2

    def own_half(value, which):
        return lax.dynamic_slice_in_dim(value, which * half, half, 1)

    grad_embeds = lax.dynamic_update_index_in_dim(grad_embeds, go(coming_grad), place(-3), 0)
    grad_embeds = grad_embeds.reshape(tokens, -1)
    other_embeds = swap(grad_embeds)
    grad_hidden = (dot_t(grad_embeds, w_out) * slope).astype(BF)
    mark(grad_hidden)
    own_hidden, own_active = own_half(grad_hidden, core), own_half(active, core)
    other_hidden = swap(own_half(grad_hidden, 1 - core))
    other_active = swap(own_half(active, 1 - core))

    def feature_term(k, hidden_now, arrived=None):
        term = dot_t(hidden_now, pick(w_in_blocks, place(k)))
        return (term if arrived is None else term + arrived.astype(F32)).astype(BF)

    held = mark(feature_term(3, go(grad_hidden)))
    coming = send(held, "y")

    starts = [(x + way * 3) % RING, (z + way * 3) % RING]
    *out_terms, low, high = mark(
        weight_terms(starts, *go(grad_embeds, other_embeds, own_active, other_active))
    )
    out_held = low, high
    *in_terms, low, high = mark(
        weight_terms(starts, *go(normed, other_normed, own_hidden, other_hidden))
    )
    in_coming, out_coming = send_all((low, high), out_held)

    held = mark(feature_term(2, *go(grad_hidden, coming)))
    coming = send(held, "y")
    embeds = (total(go(pieces)) + b_out.astype(F32)).astype(BF)
    outgoing = mark(jnp.dot(placing, embeds, preferred_element_type=F32).astype(BF))
    image_embeds = exchange(outgoing, everyone)

    in_held = mark(add_pair(in_terms, 2, go(*in_coming)))
    out_held = mark(add_pair(out_terms, 2, go(*out_coming)))
    in_coming, out_coming = send_all(in_held, out_held)

    held = mark(feature_term(1, *go(grad_hidden, coming)))
    coming = send(held, "y")
    feature = mark(feature_term(0, go(grad_hidden)))

    in_held = mark(add_pair(in_terms, 1, go(*in_coming)))
    out_held = mark(add_pair(out_terms, 1, go(*out_coming)))
    in_coming, out_coming = send_all(in_held, out_held)

    grad_normed = plus(feature, go(coming))
    scaled = grad_normed * gain
    projection = jnp.mean(scaled * merged, axis=-1, keepdims=True)
    cubed = inverse * inverse * inverse
    grad_patches = mark((inverse * scaled - merged * cubed * projection).astype(BF))

    in_low, in_high = mark(add_pair(in_terms, 0, go(*in_coming)))
    out_low, out_high = add_pair(out_terms, 0, go(*out_coming))
    low = jnp.concatenate([in_low, out_low], axis=1)
    high = jnp.concatenate([in_high, out_high], axis=1)
    low, high = lax.optimization_barrier((low, high))
    mark((low, high))

    def term(value, index, k):
        return pick(value, (index + way * k) % RING)

    arrived_low = (
        send(term(low, z, 1), "z"),
        send_across(term(low, z, 2), "z"),
        send(term(low, z, 3), "z", reverse=True),
    )
    arrived_high = (
        send(term(high, x, 1), "x"),
        send_across(term(high, x, 2), "x"),
        send(term(high, x, 3), "x", reverse=True),
    )

    def whole(own, arrived):
        return sum((piece.astype(F32) for piece in arrived), own.astype(F32)).astype(BF)

    arrived_low, arrived_high = go(arrived_low, arrived_high)
    low, high = whole(pick(low, z), arrived_low), whole(pick(high, x), arrived_high)
    other = swap(jnp.where(core == 0, high, low))
    own = jnp.where(core == 0, low, high)
    rows = jnp.where(
        core == 0,
        jnp.concatenate([own, other], axis=1),
        jnp.concatenate([other, own], axis=1),
    ).astype(F32)
    split = width // (2 * RING)
    return (image_embeds, rows[:split], rows[split:].T, grad_patches)


def solution(mesh):
    grid = Mesh(mesh.devices.reshape(RING, RING, 2, RING), ("z", "x", "c", "y"))
    enc = ("z", "x", "c")
    everyone = (*enc, "y")
    in_specs = (
        P(enc, "y"),
        P(),
        P(None, "y"),
        P("y"),
        P("y", None),
        P(),
        P(everyone, None),
        P(everyone, None),
    )
    out_specs = (P(everyone, None), P(enc, "y"), P("y", enc), P(enc, "y"))

    return jax.shard_map(
        local, mesh=grid, in_specs=in_specs, out_specs=out_specs, check_vma=False
    )
```

profile of v0, /device:TPU:0, one launch (start us, length us, event | category | flops | bytes accessed | tf_op | source)
XLA Modules:
  0.0 247.1 jit_solution(17155336333899548230)
XLA Ops:
  7.8 11.3 %all-to-all-start = ((bf16[128,2,2048]{2,1,0:T(2,128)(2,1)}), bf16[128,2,2048]{2,1,0:T(2,128)(2,1)}, u32[]{:S(2)}, u32[]{:S(2)}) async-start(bf16[128,2,2048]{2,1,0:T(2,128)(2,1)} %all_to_all.19), calls=%async_computation | async-start | bytes 2097152 | tf_op jit(solution)/shard_map/all_to_all | solution.py:39
  19.7 6.9 %shard_map.111 = (f32[512,1280]{1,0:T(8,128)}, bf16[4,512,1280]{2,1,0:T(8,128)(2,1)}) custom-call(s32[1]{0:T(128)} %bitcast.2.where, bf16[512,1280]{1,0:T(8,128)(2,1)} %copy-done.1, bf16[4,1280,1280]{2,1,0:T(8,128)(2,1)} %bitcast.113, bf16[1,1280]{1,0:T(2,128)(2,1)} %broadcast_in_dim.32.refs_0_), custom_call_target="tpu_custom_call" | custom-call | flops 1677721600 | bytes 10000000 | tf_op jit(solution)/shard_map/pallas_call | solution.py:145
  27.9 3.3 %collective-permute-start.1 = (bf16[512,1280]{1,0:T(8,128)(2,1)}, bf16[512,1280]{1,0:T(8,128)(2,1)}, u32[]{:S(2)}, u32[]{:S(2)}) collective-permute-start(bf16[512,1280]{1,0:T(8,128)(2,1)} %collective-permute-done.part), channel_id=1, source_target_pairs={{0,1},{4,7},{1,2},{5,4},{2,3},{6,5},{3,0},{7,6},{8,9},{12,15},{9,1... | collective-permute-start | bytes 3932168 | tf_op jit(solution)/shard_map/ppermute | solution.py:27
  31.4 6.5 %all-to-all-done = bf16[128,2,2048]{2,1,0:T(2,128)(2,1)} async-done(((bf16[128,2,2048]{2,1,0:T(2,128)(2,1)}), bf16[128,2,2048]{2,1,0:T(2,128)(2,1)}, u32[]{:S(2)}, u32[]{:S(2)}) %all-to-all-start) | async-done | bytes 1048608 | tf_op jit(solution)/shard_map/all_to_all | solution.py:39
  39.3 7.4 %shard_map.112 = (f32[512,1280]{1,0:T(8,128)}, bf16[4,512,1280]{2,1,0:T(8,128)(2,1)}) custom-call(s32[1]{0:T(128)} %bitcast.4.where, bf16[512,1280]{1,0:T(8,128)(2,1)} %collective-permute-done.part, bf16[4,1280,1280]{2,1,0:T(8,128)(2,1)} %bitcast.114, f32[512,1280]{1,0:T(8,128)} %get-tuple-element.77.refs_0_, ...), custom_call_target="tpu_custom_call", output_to_operand_aliasing={{1}: (4, {})} | custom-call | flops 1677721600 | bytes 10000000 | tf_op jit(solution)/shard_map/pallas_call | solution.py:145
  51.5 7.3 %shard_map.113 = (f32[512,1280]{1,0:T(8,128)}, bf16[4,512,1280]{2,1,0:T(8,128)(2,1)}) custom-call(s32[1]{0:T(128)} %bitcast.1.where, bf16[512,1280]{1,0:T(8,128)(2,1)} %collective-permute-done.1.part, bf16[4,1280,1280]{2,1,0:T(8,128)(2,1)} %bitcast.115, f32[512,1280]{1,0:T(8,128)} %get-tuple-element.81.refs_0_, ...), custom_call_target="tpu_custom_call", output_to_operand_aliasing={{1}: (4, {})} | custom-call | flops 1677721600 | bytes 10000000 | tf_op jit(solution)/shard_map/pallas_call | solution.py:145
  58.8 15.5 %collective-permute-done.3 = bf16[128,2048]{1,0:T(8,128)(2,1)S(1)} collective-permute-done((bf16[128,2048]{1,0:T(8,128)(2,1)}, bf16[128,2048]{1,0:T(8,128)(2,1)S(1)}, u32[]{:S(2)}, u32[]{:S(2)}) %collective-permute-start.3) | collective-permute-done | bytes 524320 | tf_op jit(solution)/shard_map/ppermute | solution.py:27
  76.6 7.2 %multiply_convert_fusion = (bf16[512,1280]{1,0:T(8,128)(2,1)S(1)}, f32[512,1280]{1,0:T(8,128)}) fusion(f32[512,1280]{1,0:T(8,128)} %get-tuple-element.85, bf16[512,1280]{1,0:T(8,128)(2,1)} %copy-done.6, bf16[4,1280,1280]{2,1,0:T(8,128)(2,1)} %bitcast.116, s32[]{:T(128)S(6)} %select_n.201), kind=kOutput, calls=%fused_computation.40 | convolution fusion | flops 1681653760 | bytes 11141124 | tf_op jit(solution)/shard_map/dot_general | solution.py:239
  86.0 4.1 %convolution_convert_fusion = bf16[512,2048]{1,0:T(8,128)(2,1)} fusion(bf16[512,1280]{1,0:T(8,128)(2,1)S(1)} %get-tuple-element.90, bf16[1280,2048]{1,0:T(8,128)(2,1)S(1)} %bitcast.123), kind=kOutput, calls=%fused_computation.27 | convolution fusion | flops 2685403136 | bytes 8650752 | tf_op jit(solution)/shard_map/dot_general | solution.py:250
  91.0 5.4 %collective-permute-done.5 = bf16[128,2048]{1,0:T(8,128)(2,1)S(1)} collective-permute-done((bf16[128,2048]{1,0:T(8,128)(2,1)S(1)}, bf16[128,2048]{1,0:T(8,128)(2,1)S(1)}, u32[]{:S(2)}, u32[]{:S(2)}) %collective-permute-start.5) | collective-permute-done | bytes 524320 | tf_op jit(solution)/shard_map/ppermute | solution.py:27
  99.4 6.6 %fusion.24 = bf16[512,1280]{1,0:T(8,128)(2,1)S(1)} fusion(bf16[512,2048]{1,0:T(8,128)(2,1)} %bitcast.11.own_left, bf16[1280,2048]{1,0:T(8,128)(2,1)} %param.12, f32[512,1280]{1,0:T(8,128)S(1)} %copy-done.13), kind=kOutput, calls=%fused_computation.26 | convolution fusion | flops 2690908160 | bytes 11272192 | tf_op jit(solution)/shard_map/dot_general | solution.py:51
  106.0 5.3 %fusion.12 = bf16[512,1280]{1,0:T(8,128)(2,1)} fusion(bf16[512,1280]{1,0:T(8,128)(2,1)S(1)} %fusion.24, bf16[4,1280,1280]{2,1,0:T(8,128)(2,1)} %bitcast.117, s32[]{:T(128)S(6)} %select_n.206), kind=kOutput, calls=%fused_computation.22 | convolution fusion | flops 1678376960 | bytes 5898244 | tf_op jit(solution)/shard_map/dot_general | solution.py:51
  113.1 4.2 %all-to-all-start.1 = ((bf16[4,128,2048]{2,1,0:T(8,128)(2,1)}), bf16[4,128,2048]{2,1,0:T(8,128)(2,1)S(1)}, u32[]{:S(2)}, u32[]{:S(2)}) async-start(bf16[4,128,2048]{2,1,0:T(8,128)(2,1)} %bitcast.121), calls=%async_computation.1 | async-start | bytes 4194304 | tf_op jit(solution)/shard_map/all_to_all | solution.py:39
  117.9 8.6 %shard_map.114 = (bf16[4,4,64,640]{3,2,1,0:T(8,128)(2,1)}, bf16[4,4,64,640]{3,2,1,0:T(8,128)(2,1)}, bf16[4,64,640]{2,1,0:T(8,128)(2,1)}, bf16[4,64,640]{2,1,0:T(8,128)(2,1)}) custom-call(s32[2]{0:T(128)} %pad_add_fusion.where, bf16[512,2048]{1,0:T(8,128)(2,1)} %bitcast.11.own_left, bf16[512,2048]{1,0:T(8,128)(2,1)} %collective-permute-done.9.other_left, ...), custom_call_target="tpu_custom_call" | custom-call | flops 2684354560 | bytes 20000000 | tf_op jit(solution)/shard_map/pallas_call | solution.py:100
  126.5 14.3 %shard_map.115 = (bf16[4,4,160,640]{3,2,1,0:T(8,128)(2,1)}, bf16[4,4,160,640]{3,2,1,0:T(8,128)(2,1)}, bf16[4,160,640]{2,1,0:T(8,128)(2,1)}, bf16[4,160,640]{2,1,0:T(8,128)(2,1)}) custom-call(s32[2]{0:T(128)} %pad_add_fusion.where, bf16[4,512,1280]{2,1,0:T(8,128)(2,1)} %bitcast_dynamic-update-slice_fusion.own_left, ...), custom_call_target="tpu_custom_call" | custom-call | flops 6710886400 | bytes 20000000 | tf_op jit(solution)/shard_map/pallas_call | solution.py:100
  144.8 5.7 %fusion.18 = bf16[512,1280]{1,0:T(8,128)(2,1)} fusion(bf16[512,1280]{1,0:T(8,128)(2,1)} %copy-done.4, bf16[4,1280,1280]{2,1,0:T(8,128)(2,1)} %bitcast.118, s32[]{:T(128)S(6)} %select_n.212, bf16[512,1280]{1,0:T(8,128)(2,1)} %collective-permute-done.6), kind=kOutput, calls=%fused_computation.24 | convolution fusion | flops 1679687680 | bytes 7208964 | tf_op jit(solution)/shard_map/dot_general | solution.py:51
  162.9 3.1 %collective-permute-done.14 = bf16[4,64,640]{2,1,0:T(8,128)(2,1)S(1)} collective-permute-done((bf16[4,64,640]{2,1,0:T(8,128)(2,1)}, bf16[4,64,640]{2,1,0:T(8,128)(2,1)S(1)}, u32[]{:S(2)}, u32[]{:S(2)}) %collective-permute-start.14) | collective-permute-done | bytes 327712 | tf_op jit(solution)/shard_map/ppermute | solution.py:27
  170.7 4.2 %fusion.21 = bf16[512,1280]{1,0:T(8,128)(2,1)S(1)} fusion(bf16[512,1280]{1,0:T(8,128)(2,1)S(1)} %copy-done.5, bf16[4,1280,1280]{2,1,0:T(8,128)(2,1)} %bitcast.119, s32[]{:T(128)S(6)} %select_n.224, bf16[512,1280]{1,0:T(8,128)(2,1)} %collective-permute-done.17), kind=kOutput, calls=%fused_computation.25 | convolution fusion | flops 1679687680 | bytes 7208964 | tf_op jit(solution)/shard_map/dot_general | solution.py:51
  175.0 3.8 %fusion.15 = bf16[512,1280]{1,0:T(8,128)(2,1)S(1)} fusion(bf16[512,1280]{1,0:T(8,128)(2,1)S(1)} %copy-done.5, bf16[4,1280,1280]{2,1,0:T(8,128)(2,1)} %bitcast.120, s32[]{:T(128)S(6)} %select_n.225), kind=kOutput, calls=%fused_computation.23 | convolution fusion | flops 1678376960 | bytes 5898244 | tf_op jit(solution)/shard_map/dot_general | solution.py:51
  186.9 6.9 %collective-permute-done.22 = bf16[512,1280]{1,0:T(8,128)(2,1)S(1)} collective-permute-done((bf16[512,1280]{1,0:T(8,128)(2,1)S(1)}, bf16[512,1280]{1,0:T(8,128)(2,1)S(1)}, u32[]{:S(2)}, u32[]{:S(2)}) %collective-permute-start.22) | collective-permute-done | bytes 1310752 | tf_op jit(solution)/shard_map/ppermute | solution.py:27
  204.7 3.4 %collective-permute-start.29 = (bf16[224,640]{1,0:T(8,128)(2,1)}, bf16[224,640]{1,0:T(8,128)(2,1)}, u32[]{:S(2)}, u32[]{:S(2)}) collective-permute-start(bf16[224,640]{1,0:T(8,128)(2,1)} %get-tuple-element.156), channel_id=1, source_target_pairs={{0,16},{8,24},{16,0},{24,8},{1,17},{9,25},{17,1},{25,9},{2,18},{10... | collective-permute-start | bytes 860168 | tf_op jit(solution)/shard_map/ppermute | solution.py:31
  211.3 4.9 %collective-permute-done.28 = bf16[224,640]{1,0:T(8,128)(2,1)} collective-permute-done((bf16[224,640]{1,0:T(8,128)(2,1)}, bf16[224,640]{1,0:T(8,128)(2,1)}, u32[]{:S(2)}, u32[]{:S(2)}) %collective-permute-start.28) | collective-permute-done | bytes 286752 | tf_op jit(solution)/shard_map/ppermute | solution.py:27
  220.2 5.3 %all-to-all-start.2 = ((bf16[128,2,2048]{2,1,0:T(2,128)(2,1)}), bf16[128,2,2048]{2,1,0:T(2,128)(2,1)S(1)}, u32[]{:S(2)}, u32[]{:S(2)}) async-start(bf16[128,2,2048]{2,1,0:T(2,128)(2,1)} %all_to_all.23), calls=%async_computation.2 | async-start | bytes 2097152 | tf_op jit(solution)/shard_map/all_to_all | solution.py:39
  228.1 16.0 %all-to-all-done.2 = bf16[128,2,2048]{2,1,0:T(2,128)(2,1)S(1)} async-done(((bf16[128,2,2048]{2,1,0:T(2,128)(2,1)}), bf16[128,2,2048]{2,1,0:T(2,128)(2,1)S(1)}, u32[]{:S(2)}, u32[]{:S(2)}) %all-to-all-start.2) | async-done | bytes 1048608 | tf_op jit(solution)/shard_map/all_to_all | solution.py:39
  (137 shorter events, 78.9 us)
Async XLA Ops:
  3.5 24.4 %collective-permute-start = (bf16[512,1280]{1,0:T(8,128)(2,1)S(1)}, bf16[512,1280]{1,0:T(8,128)(2,1)}, u32[]{:S(2)}, u32[]{:S(2)}) collective-permute-start(bf16[512,1280]{1,0:T(8,128)(2,1)S(1)} %fusion.31.part), channel_id=1, source_target_pairs={{0,1},{4,7},{1,2},{5,4},{2,3},{6,5},{3,0},{7,6},{8,9},{12,15},{9,1... | collective-permute-start | bytes 3932168 | tf_op jit(solution)/shard_map/ppermute | solution.py:27
  7.8 30.1 %all-to-all-start = ((bf16[128,2,2048]{2,1,0:T(2,128)(2,1)}), bf16[128,2,2048]{2,1,0:T(2,128)(2,1)}, u32[]{:S(2)}, u32[]{:S(2)}) async-start(bf16[128,2,2048]{2,1,0:T(2,128)(2,1)} %all_to_all.19), calls=%async_computation | async-start | bytes 2097152 | tf_op jit(solution)/shard_map/all_to_all | solution.py:39
  27.9 21.7 %collective-permute-start.1 = (bf16[512,1280]{1,0:T(8,128)(2,1)}, bf16[512,1280]{1,0:T(8,128)(2,1)}, u32[]{:S(2)}, u32[]{:S(2)}) collective-permute-start(bf16[512,1280]{1,0:T(8,128)(2,1)} %collective-permute-done.part), channel_id=1, source_target_pairs={{0,1},{4,7},{1,2},{5,4},{2,3},{6,5},{3,0},{7,6},{8,9},{12,15},{9,1... | collective-permute-start | bytes 3932168 | tf_op jit(solution)/shard_map/ppermute | solution.py:27
  49.6 24.6 %collective-permute-start.2 = (bf16[512,1280]{1,0:T(8,128)(2,1)}, bf16[512,1280]{1,0:T(8,128)(2,1)S(1)}, u32[]{:S(2)}, u32[]{:S(2)}) collective-permute-start(bf16[512,1280]{1,0:T(8,128)(2,1)} %collective-permute-done.1.part), channel_id=1, source_target_pairs={{0,1},{4,7},{1,2},{5,4},{2,3},{6,5},{3,0},{7,6},{8,9},{12,15},{9,1... | collective-permute-start | bytes 3932168 | tf_op jit(solution)/shard_map/ppermute | solution.py:27
  49.6 24.6 %collective-permute-start.3 = (bf16[128,2048]{1,0:T(8,128)(2,1)}, bf16[128,2048]{1,0:T(8,128)(2,1)S(1)}, u32[]{:S(2)}, u32[]{:S(2)}) collective-permute-start(bf16[128,2048]{1,0:T(8,128)(2,1)} %get-tuple-element.166), channel_id=1, source_target_pairs={{0,1},{4,7},{1,2},{5,4},{2,3},{6,5},{3,0},{7,6},{8,9},{12,15},{9,1... | collective-permute-start | bytes 1572872 | tf_op jit(solution)/shard_map/ppermute | solution.py:27
  75.6 50.9 %collective-permute-start.7 = (bf16[4,512,1280]{2,1,0:T(8,128)(2,1)}, bf16[4,512,1280]{2,1,0:T(8,128)(2,1)}, u32[]{:S(2)}, u32[]{:S(2)}) collective-permute-start(bf16[4,512,1280]{2,1,0:T(8,128)(2,1)} %bitcast_dynamic-update-slice_fusion.own_left), channel_id=1, source_target_pairs={{0,4},{4,0},{1,5},{5,1},{2,6},{6,2},{3,7},{7,3},{8,12},{12,8},{9,1... | collective-permute-start | bytes 15728648 | tf_op jit(solution)/shard_map/ppermute | solution.py:35
  97.2 20.7 %collective-permute-start.9 = (bf16[512,2048]{1,0:T(8,128)(2,1)}, bf16[512,2048]{1,0:T(8,128)(2,1)}, u32[]{:S(2)}, u32[]{:S(2)}) collective-permute-start(bf16[512,2048]{1,0:T(8,128)(2,1)} %bitcast.11.own_left), channel_id=1, source_target_pairs={{0,4},{4,0},{1,5},{5,1},{2,6},{6,2},{3,7},{7,3},{8,12},{12,8},{9,1... | collective-permute-start | bytes 6291464 | tf_op jit(solution)/shard_map/ppermute | solution.py:35
  98.4 19.5 %collective-permute-start.10 = (bf16[512,640]{1,0:T(8,128)(2,1)}, bf16[512,640]{1,0:T(8,128)(2,1)}, u32[]{:S(2)}, u32[]{:S(2)}) collective-permute-start(bf16[512,640]{1,0:T(8,128)(2,1)} %get-tuple-element.151), channel_id=1, source_target_pairs={{0,4},{4,0},{1,5},{5,1},{2,6},{6,2},{3,7},{7,3},{8,12},{12,8},{9,1... | collective-permute-start | bytes 1966088 | tf_op jit(solution)/shard_map/ppermute | solution.py:35
  111.4 33.4 %collective-permute-start.6 = (bf16[512,1280]{1,0:T(8,128)(2,1)}, bf16[512,1280]{1,0:T(8,128)(2,1)}, u32[]{:S(2)}, u32[]{:S(2)}) collective-permute-start(bf16[512,1280]{1,0:T(8,128)(2,1)} %fusion.12), channel_id=1, source_target_pairs={{0,1},{4,7},{1,2},{5,4},{2,3},{6,5},{3,0},{7,6},{8,9},{12,15},{9,1... | collective-permute-start | bytes 3932168 | tf_op jit(solution)/shard_map/ppermute | solution.py:27
  113.1 39.8 %all-to-all-start.1 = ((bf16[4,128,2048]{2,1,0:T(8,128)(2,1)}), bf16[4,128,2048]{2,1,0:T(8,128)(2,1)S(1)}, u32[]{:S(2)}, u32[]{:S(2)}) async-start(bf16[4,128,2048]{2,1,0:T(8,128)(2,1)} %bitcast.121), calls=%async_computation.1 | async-start | bytes 4194304 | tf_op jit(solution)/shard_map/all_to_all | solution.py:39
  140.8 17.2 %collective-permute-start.11 = (bf16[4,160,640]{2,1,0:T(8,128)(2,1)}, bf16[4,160,640]{2,1,0:T(8,128)(2,1)}, u32[]{:S(2)}, u32[]{:S(2)}) collective-permute-start(bf16[4,160,640]{2,1,0:T(8,128)(2,1)} %get-tuple-element.112), channel_id=1, source_target_pairs={{0,8},{4,28},{8,16},{12,4},{16,24},{20,12},{24,0},{28,20},{1,9},{5... | collective-permute-start | bytes 2457608 | tf_op jit(solution)/shard_map/ppermute | solution.py:27
  142.9 16.0 %collective-permute-start.12 = (bf16[4,160,640]{2,1,0:T(8,128)(2,1)}, bf16[4,160,640]{2,1,0:T(8,128)(2,1)}, u32[]{:S(2)}, u32[]{:S(2)}) collective-permute-start(bf16[4,160,640]{2,1,0:T(8,128)(2,1)} %get-tuple-element.113), channel_id=1, source_target_pairs={{0,32},{4,100},{32,64},{36,4},{64,96},{68,36},{96,0},{100,68},{1,3... | collective-permute-start | bytes 2457608 | tf_op jit(solution)/shard_map/ppermute | solution.py:27
  150.5 20.3 %collective-permute-start.17 = (bf16[512,1280]{1,0:T(8,128)(2,1)}, bf16[512,1280]{1,0:T(8,128)(2,1)}, u32[]{:S(2)}, u32[]{:S(2)}) collective-permute-start(bf16[512,1280]{1,0:T(8,128)(2,1)} %fusion.18), channel_id=1, source_target_pairs={{0,1},{4,7},{1,2},{5,4},{2,3},{6,5},{3,0},{7,6},{8,9},{12,15},{9,1... | collective-permute-start | bytes 3932168 | tf_op jit(solution)/shard_map/ppermute | solution.py:27
  167.7 15.7 %collective-permute-start.18 = (bf16[4,64,640]{2,1,0:T(8,128)(2,1)S(1)}, bf16[4,64,640]{2,1,0:T(8,128)(2,1)S(1)}, u32[]{:S(2)}, u32[]{:S(2)}) collective-permute-start(bf16[4,64,640]{2,1,0:T(8,128)(2,1)S(1)} %fusion.47), channel_id=1, source_target_pairs={{0,8},{4,28},{8,16},{12,4},{16,24},{20,12},{24,0},{28,20},{1,9},{5... | collective-permute-start | bytes 983048 | tf_op jit(solution)/shard_map/ppermute | solution.py:27
  168.9 15.8 %collective-permute-start.19 = (bf16[4,64,640]{2,1,0:T(8,128)(2,1)S(1)}, bf16[4,64,640]{2,1,0:T(8,128)(2,1)S(1)}, u32[]{:S(2)}, u32[]{:S(2)}) collective-permute-start(bf16[4,64,640]{2,1,0:T(8,128)(2,1)S(1)} %fusion.46), channel_id=1, source_target_pairs={{0,32},{4,100},{32,64},{36,4},{64,96},{68,36},{96,0},{100,68},{1,3... | collective-permute-start | bytes 983048 | tf_op jit(solution)/shard_map/ppermute | solution.py:27
  174.9 18.9 %collective-permute-start.22 = (bf16[512,1280]{1,0:T(8,128)(2,1)S(1)}, bf16[512,1280]{1,0:T(8,128)(2,1)S(1)}, u32[]{:S(2)}, u32[]{:S(2)}) collective-permute-start(bf16[512,1280]{1,0:T(8,128)(2,1)S(1)} %fusion.21), channel_id=1, source_target_pairs={{0,1},{4,7},{1,2},{5,4},{2,3},{6,5},{3,0},{7,6},{8,9},{12,15},{9,1... | collective-permute-start | bytes 3932168 | tf_op jit(solution)/shard_map/ppermute | solution.py:27
  186.2 15.8 %collective-permute-start.23 = (bf16[4,64,640]{2,1,0:T(8,128)(2,1)S(1)}, bf16[4,64,640]{2,1,0:T(8,128)(2,1)S(1)}, u32[]{:S(2)}, u32[]{:S(2)}) collective-permute-start(bf16[4,64,640]{2,1,0:T(8,128)(2,1)S(1)} %fusion.45), channel_id=1, source_target_pairs={{0,8},{4,28},{8,16},{12,4},{16,24},{20,12},{24,0},{28,20},{1,9},{5... | collective-permute-start | bytes 983048 | tf_op jit(solution)/shard_map/ppermute | solution.py:27
  186.4 16.9 %collective-permute-start.24 = (bf16[4,64,640]{2,1,0:T(8,128)(2,1)S(1)}, bf16[4,64,640]{2,1,0:T(8,128)(2,1)S(1)}, u32[]{:S(2)}, u32[]{:S(2)}) collective-permute-start(bf16[4,64,640]{2,1,0:T(8,128)(2,1)S(1)} %fusion.44), channel_id=1, source_target_pairs={{0,32},{4,100},{32,64},{36,4},{64,96},{68,36},{96,0},{100,68},{1,3... | collective-permute-start | bytes 983048 | tf_op jit(solution)/shard_map/ppermute | solution.py:27
  204.7 20.7 %collective-permute-start.29 = (bf16[224,640]{1,0:T(8,128)(2,1)}, bf16[224,640]{1,0:T(8,128)(2,1)}, u32[]{:S(2)}, u32[]{:S(2)}) collective-permute-start(bf16[224,640]{1,0:T(8,128)(2,1)} %get-tuple-element.156), channel_id=1, source_target_pairs={{0,16},{8,24},{16,0},{24,8},{1,17},{9,25},{17,1},{25,9},{2,18},{10... | collective-permute-start | bytes 860168 | tf_op jit(solution)/shard_map/ppermute | solution.py:31
  208.1 17.4 %collective-permute-start.30 = (bf16[224,640]{1,0:T(8,128)(2,1)}, bf16[224,640]{1,0:T(8,128)(2,1)}, u32[]{:S(2)}, u32[]{:S(2)}) collective-permute-start(bf16[224,640]{1,0:T(8,128)(2,1)} %get-tuple-element.155), channel_id=1, source_target_pairs={{0,24},{4,12},{8,0},{12,20},{16,8},{20,28},{24,16},{28,4},{1,25},{... | collective-permute-start | bytes 860168 | tf_op jit(solution)/shard_map/ppermute | solution.py:27
  210.3 15.2 %collective-permute-start.25 = (bf16[224,640]{1,0:T(8,128)(2,1)}, bf16[224,640]{1,0:T(8,128)(2,1)}, u32[]{:S(2)}, u32[]{:S(2)}) collective-permute-start(bf16[224,640]{1,0:T(8,128)(2,1)} %get-tuple-element.160), channel_id=1, source_target_pairs={{0,32},{4,100},{32,64},{36,4},{64,96},{68,36},{96,0},{100,68},{1,3... | collective-permute-start | bytes 860168 | tf_op jit(solution)/shard_map/ppermute | solution.py:27
  210.3 15.2 %collective-permute-start.26 = (bf16[224,640]{1,0:T(8,128)(2,1)}, bf16[224,640]{1,0:T(8,128)(2,1)}, u32[]{:S(2)}, u32[]{:S(2)}) collective-permute-start(bf16[224,640]{1,0:T(8,128)(2,1)} %get-tuple-element.159), channel_id=1, source_target_pairs={{0,64},{32,96},{64,0},{96,32},{1,65},{33,97},{65,1},{97,33},{2,66}... | collective-permute-start | bytes 860168 | tf_op jit(solution)/shard_map/ppermute | solution.py:31
  220.2 23.9 %all-to-all-start.2 = ((bf16[128,2,2048]{2,1,0:T(2,128)(2,1)}), bf16[128,2,2048]{2,1,0:T(2,128)(2,1)S(1)}, u32[]{:S(2)}, u32[]{:S(2)}) async-start(bf16[128,2,2048]{2,1,0:T(2,128)(2,1)} %all_to_all.23), calls=%async_computation.2 | async-start | bytes 2097152 | tf_op jit(solution)/shard_map/all_to_all | solution.py:39
  228.0 17.3 %collective-permute-start.31 = (bf16[224,640]{1,0:T(8,128)(2,1)S(1)}, bf16[224,640]{1,0:T(8,128)(2,1)S(1)}, u32[]{:S(2)}, u32[]{:S(2)}) collective-permute-start(bf16[224,640]{1,0:T(8,128)(2,1)S(1)} %broadcast_select_fusion), channel_id=1, source_target_pairs={{0,4},{4,0},{1,5},{5,1},{2,6},{6,2},{3,7},{7,3},{8,12},{12,8},{9,1... | collective-permute-start | bytes 860168 | tf_op jit(solution)/shard_map/ppermute | solution.py:35
  (27 other events, 262.9 us)
where the time goes:
time: 249 us; the launch traced here: 247 us
  waiting for transfers between devices  76.1 us (31%)
  starting transfers between devices  53.7 us (22%)
  Pallas kernels  44.4 us (18%)
  matrix products  38.7 us (16%)
  local copies, waits for them, and re-layouts  19.5 us (8%)
  other arithmetic  13.7 us (6%)
    ppermute x25, waiting for transfers between devices, send(): lax.ppermute(value, ('c', 'y') if axis == 'y' else (axis, 'c'), pairs)  53.2 us
    ppermute x25, starting transfers between devices, send(): lax.ppermute(value, ('c', 'y') if axis == 'y' else (axis, 'c'), pairs)  27.6 us
    dot_general x5, matrix products, dot_t(): lax.dot_general(left, right, (((1,), (1,)), ((), ())), preferred_element_...  25.6 us
    all_to_all x3, waiting for transfers between devices, exchange(): return lax.all_to_all(value, axis, 0, 0, tiled=True)  22.9 us
    pallas_call x2, Pallas kernels, weight_terms(): pl.pallas_call(weight_kernel, grid_spec=pltpu.PrefetchScalarGridSpec(num_...  22.8 us
    pallas_call x3, Pallas kernels, hidden_terms(): pl.pallas_call(hidden_kernel, grid_spec=pltpu.PrefetchScalarGridSpec(num_...  21.6 us
    all_to_all x3, starting transfers between devices, exchange(): return lax.all_to_all(value, axis, 0, 0, tiled=True)  20.7 us
    dot_general x1, matrix products, local(): jnp.dot(part, pick(w_in_blocks, place(-3)), preferred_element_type=F32)  7.19 us
  transfers between devices with their start and end apart: 35, of which 20 were waited for; matrix products, arithmetic and copies ran while one was open for 23% of the time, Pallas kernels for 18%

commit v1 on v0

--- a/solution.py
+++ b/solution.py
@@ -121,16 +121,8 @@
 
 def hidden_kernel(where, part, weights, *refs):
     *earlier, out, filed = refs
-    held = earlier[0]
-    rows = part.shape[0] // 4
-
-    def one(i, carry):
-        cut = pl.ds(pl.multiple_of(i * rows, rows), rows)
-        term = jnp.dot(part[cut], weights[0], preferred_element_type=F32)
-        out[cut] = term + (held[...] if held.shape[0] == 1 else held[cut]).astype(F32)
-        return carry
-
-    lax.fori_loop(0, 4, one, 0)
+    term = jnp.dot(part[...], weights[0], preferred_element_type=F32)
+    out[...] = term + earlier[0][...].astype(F32)
 
     @pl.when(pl.program_id(0) == 0)
     def _():
@@ -230,26 +222,26 @@
     grad_embeds = lax.dynamic_update_index_in_dim(grad_embeds, part_grad, y, 0)
     part = mark(go(coming))
     coming = send(part, "y")
-    hidden, normed = mark(hidden_terms(place(-2), part, w_in_blocks, hidden, normed))
     part_grad = mark(go(coming_grad))
     coming_grad = send(part_grad, "y")
     grad_embeds = lax.dynamic_update_index_in_dim(grad_embeds, part_grad, place(-1), 0)
-    part = mark(go(coming))
+    hidden, normed = mark(
+        hidden_terms(place(-2), go(part), w_in_blocks, hidden, normed)
+    )
+    part_grad = mark(go(coming_grad))
+    coming_grad = send(part_grad, "y")
+    grad_embeds = lax.dynamic_update_index_in_dim(grad_embeds, part_grad, place(-2), 0)
+    mark(grad_embeds)
+    part = go(coming)
     normed = lax.dynamic_update_index_in_dim(normed, part, place(-3), 0)
     hidden = hidden + jnp.dot(
         part, pick(w_in_blocks, place(-3)), preferred_element_type=F32
     )
-    other_normed = swap(normed)
     cdf = 0.5 * (1.0 + lax.erf(hidden * HALF_ROOT))
     active = mark((hidden * cdf).astype(BF))
     slope = cdf + hidden * jnp.exp(-0.5 * hidden * hidden) * DENSITY
 
-    part_grad = mark(go(coming_grad))
-    coming_grad = send(part_grad, "y")
-    grad_embeds = lax.dynamic_update_index_in_dim(grad_embeds, part_grad, place(-2), 0)
-    partial = jnp.dot(go(active), w_out, preferred_element_type=F32).astype(BF)
-    mark(partial)
-    pieces = exchange(partial.reshape(RING, own_rows, -1), "y")
+    other_normed = swap(go(normed))
     half = active.shape[1] // 2
 
     def own_half(value, which):
@@ -258,8 +250,7 @@
     grad_embeds = lax.dynamic_update_index_in_dim(grad_embeds, go(coming_grad), place(-3), 0)
     grad_embeds = grad_embeds.reshape(tokens, -1)
     other_embeds = swap(grad_embeds)
-    grad_hidden = (dot_t(grad_embeds, w_out) * slope).astype(BF)
-    mark(grad_hidden)
+    grad_hidden = mark((dot_t(grad_embeds, w_out) * slope).astype(BF))
     own_hidden, own_active = own_half(grad_hidden, core), own_half(active, core)
     other_hidden = swap(own_half(grad_hidden, 1 - core))
     other_active = swap(own_half(active, 1 - core))
@@ -283,27 +274,24 @@
 
     held = mark(feature_term(2, *go(grad_hidden, coming)))
     coming = send(held, "y")
+    partial = mark(jnp.dot(go(active), w_out, preferred_element_type=F32).astype(BF))
+    pieces = exchange(partial.reshape(RING, own_rows, -1), "y")
+
+    in_held = mark(add_pair(in_terms, 2, go(*in_coming)))
+    out_held = mark(add_pair(out_terms, 2, go(*out_coming)))
+    in_coming, out_coming = send_all(in_held, out_held)
+
+    held = mark(feature_term(1, *go(grad_hidden, coming)))
+    coming = send(held, "y")
+    feature = mark(feature_term(0, go(grad_hidden)))
+
+    in_held = mark(add_pair(in_terms, 1, go(*in_coming)))
+    out_held = mark(add_pair(out_terms, 1, go(*out_coming)))
+    in_coming, out_coming = send_all(in_held, out_held)
+
     embeds = (total(go(pieces)) + b_out.astype(F32)).astype(BF)
     outgoing = mark(jnp.dot(placing, embeds, preferred_element_type=F32).astype(BF))
     image_embeds = exchange(outgoing, everyone)
-
-    in_held = mark(add_pair(in_terms, 2, go(*in_coming)))
-    out_held = mark(add_pair(out_terms, 2, go(*out_coming)))
-    in_coming, out_coming = send_all(in_held, out_held)
-
-    held = mark(feature_term(1, *go(grad_hidden, coming)))
-    coming = send(held, "y")
-    feature = mark(feature_term(0, go(grad_hidden)))
-
-    in_held = mark(add_pair(in_terms, 1, go(*in_coming)))
-    out_held = mark(add_pair(out_terms, 1, go(*out_coming)))
-    in_coming, out_coming = send_all(in_held, out_held)
-
-    grad_normed = plus(feature, go(coming))
-    scaled = grad_normed * gain
-    projection = jnp.mean(scaled * merged, axis=-1, keepdims=True)
-    cubed = inverse * inverse * inverse
-    grad_patches = mark((inverse * scaled - merged * cubed * projection).astype(BF))
 
     in_low, in_high = mark(add_pair(in_terms, 0, go(*in_coming)))
     out_low, out_high = add_pair(out_terms, 0, go(*out_coming))
@@ -325,6 +313,12 @@
         send_across(term(high, x, 2), "x"),
         send(term(high, x, 3), "x", reverse=True),
     )
+
+    grad_normed = plus(feature, go(coming))
+    scaled = grad_normed * gain
+    projection = jnp.mean(scaled * merged, axis=-1, keepdims=True)
+    cubed = inverse * inverse * inverse
+    grad_patches = mark((inverse * scaled - merged * cubed * projection).astype(BF))
 
     def whole(own, arrived):
         return sum((piece.astype(F32) for piece in arrived), own.astype(F32)).astype(BF)

time: 249 us -> 244 us (0.980)
  waiting for transfers between devices: 76.1 us -> 51.7 us
  other arithmetic: 13.7 us -> 26.3 us
  starting transfers between devices: 53.7 us -> 60.9 us
  matrix products: 38.7 us -> 41.8 us
  Pallas kernels: 44.4 us -> 41.5 us
    all_to_all x3, waiting for transfers between devices: 22.9 us -> 6.46 us  [exchange(): return lax.all_to_all(value, axis, 0, 0, tiled=True)]
    convert_element_type x11, other arithmetic: 4.26 us -> 16.3 us  [add_pair(): return (low.astype(BF), high.astype(BF))]
    ppermute x25, waiting for transfers between devices: 53.2 us -> 44.9 us  [send(): lax.ppermute(value, ('c', 'y') if axis == 'y' else (axis, 'c'), pairs)]
    ppermute x25, starting transfers between devices: 27.6 us -> 31.1 us  [send(): lax.ppermute(value, ('c', 'y') if axis == 'y' else (axis, 'c'), pairs)]
    pallas_call x3, Pallas kernels: 21.6 us -> 18.5 us  [hidden_terms(): pl.pallas_call(hidden_kernel, grid_spec=pltpu.PrefetchScalarGridSpec(num_...]
  transfers between devices with their start and end apart: 35 -> 35, of which waited for: 20 -> 10; matrix products, arithmetic and copies ran while one was open for 23% -> 27% of each run, Pallas kernels for 18% -> 17%
where the time goes in v1:
time: 244 us; the launch traced here: 242 us
  starting transfers between devices  60.9 us (25%)
  waiting for transfers between devices  51.7 us (21%)
  matrix products  41.8 us (17%)
  Pallas kernels  41.5 us (17%)
  other arithmetic  26.3 us (11%)
  local copies, waits for them, and re-layouts  18.4 us (8%)
    ppermute x25, waiting for transfers between devices, send(): lax.ppermute(value, ('c', 'y') if axis == 'y' else (axis, 'c'), pairs)  44.9 us
    ppermute x25, starting transfers between devices, send(): lax.ppermute(value, ('c', 'y') if axis == 'y' else (axis, 'c'), pairs)  31.1 us
    dot_general x5, matrix products, dot_t(): lax.dot_general(left, right, (((1,), (1,)), ((), ())), preferred_element_...  27.4 us
    all_to_all x3, starting transfers between devices, exchange(): return lax.all_to_all(value, axis, 0, 0, tiled=True)  23.2 us
    pallas_call x2, Pallas kernels, weight_terms(): pl.pallas_call(weight_kernel, grid_spec=pltpu.PrefetchScalarGridSpec(num_...  23 us
    pallas_call x3, Pallas kernels, hidden_terms(): pl.pallas_call(hidden_kernel, grid_spec=pltpu.PrefetchScalarGridSpec(num_...  18.5 us
    convert_element_type x11, other arithmetic, add_pair(): return (low.astype(BF), high.astype(BF))  16.3 us
    dot_general x1, matrix products, local(): jnp.dot(part, pick(w_in_blocks, place(-3)), preferred_element_type=F32)  7.04 us
  transfers between devices with their start and end apart: 35, of which 10 were waited for; matrix products, arithmetic and copies ran while one was open for 27% of the time, Pallas kernels for 17%

profile of v1, /device:TPU:0, one launch (start us, length us, event | category | flops | bytes accessed | tf_op | source)
XLA Modules:
  0.0 241.7 jit_solution(13666394017291033574)
XLA Ops:
  7.8 11.3 %all-to-all-start = ((bf16[128,2,2048]{2,1,0:T(2,128)(2,1)}), bf16[128,2,2048]{2,1,0:T(2,128)(2,1)}, u32[]{:S(2)}, u32[]{:S(2)}) async-start(bf16[128,2,2048]{2,1,0:T(2,128)(2,1)} %all_to_all.19), calls=%async_computation | async-start | bytes 2097152 | tf_op jit(solution)/shard_map/all_to_all | solution.py:39
  19.7 5.9 %shard_map.111 = (f32[512,1280]{1,0:T(8,128)}, bf16[4,512,1280]{2,1,0:T(8,128)(2,1)}) custom-call(s32[1]{0:T(128)} %bitcast.2.where, bf16[512,1280]{1,0:T(8,128)(2,1)} %copy-done.2, bf16[4,1280,1280]{2,1,0:T(8,128)(2,1)} %bitcast.113, bf16[1,1280]{1,0:T(2,128)(2,1)} %broadcast_in_dim.32.refs_0_), custom_call_target="tpu_custom_call" | custom-call | flops 1677721600 | bytes 10000000 | tf_op jit(solution)/shard_map/pallas_call | solution.py:137
  27.9 3.3 %collective-permute-start.1 = (bf16[512,1280]{1,0:T(8,128)(2,1)}, bf16[512,1280]{1,0:T(8,128)(2,1)}, u32[]{:S(2)}, u32[]{:S(2)}) collective-permute-start(bf16[512,1280]{1,0:T(8,128)(2,1)} %collective-permute-done.part), channel_id=1, source_target_pairs={{0,1},{4,7},{1,2},{5,4},{2,3},{6,5},{3,0},{7,6},{8,9},{12,15},{9,1... | collective-permute-start | bytes 3932168 | tf_op jit(solution)/shard_map/ppermute | solution.py:27
  31.4 6.5 %all-to-all-done = bf16[128,2,2048]{2,1,0:T(2,128)(2,1)} async-done(((bf16[128,2,2048]{2,1,0:T(2,128)(2,1)}), bf16[128,2,2048]{2,1,0:T(2,128)(2,1)}, u32[]{:S(2)}, u32[]{:S(2)}) %all-to-all-start) | async-done | bytes 1048608 | tf_op jit(solution)/shard_map/all_to_all | solution.py:39
  39.3 6.3 %shard_map.112 = (f32[512,1280]{1,0:T(8,128)}, bf16[4,512,1280]{2,1,0:T(8,128)(2,1)}) custom-call(s32[1]{0:T(128)} %bitcast.4.where, bf16[512,1280]{1,0:T(8,128)(2,1)} %collective-permute-done.part, bf16[4,1280,1280]{2,1,0:T(8,128)(2,1)} %bitcast.114, f32[512,1280]{1,0:T(8,128)} %get-tuple-element.79.refs_0_, ...), custom_call_target="tpu_custom_call", output_to_operand_aliasing={{1}: (4, {})} | custom-call | flops 1677721600 | bytes 10000000 | tf_op jit(solution)/shard_map/pallas_call | solution.py:137
  49.1 9.0 %collective-permute-done.2 = bf16[128,2048]{1,0:T(8,128)(2,1)} collective-permute-done((bf16[128,2048]{1,0:T(8,128)(2,1)S(1)}, bf16[128,2048]{1,0:T(8,128)(2,1)}, u32[]{:S(2)}, u32[]{:S(2)}) %collective-permute-start.2) | collective-permute-done | bytes 524320 | tf_op jit(solution)/shard_map/ppermute | solution.py:27
  58.2 6.4 %shard_map.113 = (f32[512,1280]{1,0:T(8,128)}, bf16[4,512,1280]{2,1,0:T(8,128)(2,1)}) custom-call(s32[1]{0:T(128)} %bitcast.1.where, bf16[512,1280]{1,0:T(8,128)(2,1)} %collective-permute-done.1.part, bf16[4,1280,1280]{2,1,0:T(8,128)(2,1)} %bitcast.115, f32[512,1280]{1,0:T(8,128)} %get-tuple-element.83.refs_0_, ...), custom_call_target="tpu_custom_call", output_to_operand_aliasing={{1}: (4, {})} | custom-call | flops 1677721600 | bytes 10000000 | tf_op jit(solution)/shard_map/pallas_call | solution.py:137
  65.6 12.2 %collective-permute-done.4 = bf16[128,2048]{1,0:T(8,128)(2,1)} collective-permute-done((bf16[128,2048]{1,0:T(8,128)(2,1)}, bf16[128,2048]{1,0:T(8,128)(2,1)}, u32[]{:S(2)}, u32[]{:S(2)}) %collective-permute-start.4) | collective-permute-done | bytes 524320 | tf_op jit(solution)/shard_map/ppermute | solution.py:27
  78.9 7.0 %multiply_convert_fusion = (bf16[512,1280]{1,0:T(8,128)(2,1)}, f32[512,1280]{1,0:T(8,128)}) fusion(f32[512,1280]{1,0:T(8,128)} %get-tuple-element.89, bf16[512,1280]{1,0:T(8,128)(2,1)} %collective-permute-done.3, bf16[4,1280,1280]{2,1,0:T(8,128)(2,1)} %bitcast.116, s32[]{:T(128)S(6)} %select_n.204), kind=kOutput, calls=%fused_computation.40 | convolution fusion | flops 1681653760 | bytes 11141124 | tf_op jit(solution)/shard_map/dot_general | solution.py:237
  88.4 10.6 %collective-permute-done.5 = bf16[128,2048]{1,0:T(8,128)(2,1)S(1)} collective-permute-done((bf16[128,2048]{1,0:T(8,128)(2,1)}, bf16[128,2048]{1,0:T(8,128)(2,1)S(1)}, u32[]{:S(2)}, u32[]{:S(2)}) %collective-permute-start.5) | collective-permute-done | bytes 524320 | tf_op jit(solution)/shard_map/ppermute | solution.py:27
  99.4 7.0 %fusion.24 = bf16[512,1280]{1,0:T(8,128)(2,1)S(1)} fusion(bf16[512,2048]{1,0:T(8,128)(2,1)S(1)} %bitcast.122, bf16[1280,2048]{1,0:T(8,128)(2,1)} %param.12, f32[512,1280]{1,0:T(8,128)} %get-tuple-element.170), kind=kOutput, calls=%fused_computation.26 | convolution fusion | flops 2690908160 | bytes 11272192 | tf_op jit(solution)/shard_map/dot_general | solution.py:51
  107.9 4.9 %fusion.12 = bf16[512,1280]{1,0:T(8,128)(2,1)} fusion(bf16[512,1280]{1,0:T(8,128)(2,1)S(1)} %fusion.24, bf16[4,1280,1280]{2,1,0:T(8,128)(2,1)} %bitcast.117, s32[]{:T(128)S(6)} %select_n.206), kind=kOutput, calls=%fused_computation.22 | convolution fusion | flops 1678376960 | bytes 5898244 | tf_op jit(solution)/shard_map/dot_general | solution.py:51
  115.2 8.6 %shard_map.114 = (bf16[4,4,64,640]{3,2,1,0:T(8,128)(2,1)}, bf16[4,4,64,640]{3,2,1,0:T(8,128)(2,1)}, bf16[4,64,640]{2,1,0:T(8,128)(2,1)}, bf16[4,64,640]{2,1,0:T(8,128)(2,1)}) custom-call(s32[2]{0:T(128)} %pad_add_fusion.where, bf16[512,2048]{1,0:T(8,128)(2,1)} %bitcast.123, bf16[512,2048]{1,0:T(8,128)(2,1)} %collective-permute-done.9.other_left, ...), custom_call_target="tpu_custom_call" | custom-call | flops 2684354560 | bytes 20000000 | tf_op jit(solution)/shard_map/pallas_call | solution.py:100
  123.8 14.4 %shard_map.115 = (bf16[4,4,160,640]{3,2,1,0:T(8,128)(2,1)}, bf16[4,4,160,640]{3,2,1,0:T(8,128)(2,1)}, bf16[4,160,640]{2,1,0:T(8,128)(2,1)}, bf16[4,160,640]{2,1,0:T(8,128)(2,1)}) custom-call(s32[2]{0:T(128)} %pad_add_fusion.where, bf16[4,512,1280]{2,1,0:T(8,128)(2,1)} %bitcast_dynamic-update-slice_fusion.own_left, ...), custom_call_target="tpu_custom_call" | custom-call | flops 6710886400 | bytes 20000000 | tf_op jit(solution)/shard_map/pallas_call | solution.py:100
  140.7 5.4 %fusion.18 = bf16[512,1280]{1,0:T(8,128)(2,1)} fusion(bf16[512,1280]{1,0:T(8,128)(2,1)S(1)} %copy-done.9, bf16[4,1280,1280]{2,1,0:T(8,128)(2,1)} %bitcast.118, s32[]{:T(128)S(6)} %select_n.212, bf16[512,1280]{1,0:T(8,128)(2,1)} %collective-permute-done.6), kind=kOutput, calls=%fused_computation.24 | convolution fusion | flops 1679687680 | bytes 7208964 | tf_op jit(solution)/shard_map/dot_general | solution.py:51
  147.8 6.5 %convolution_convert_fusion = bf16[512,2048]{1,0:T(8,128)(2,1)} fusion(bf16[512,1280]{1,0:T(8,128)(2,1)S(1)} %copy-done.7, bf16[1280,2048]{1,0:T(8,128)(2,1)} %param.12), kind=kOutput, calls=%fused_computation.27 | convolution fusion | flops 2685403136 | bytes 8650752 | tf_op jit(solution)/shard_map/dot_general | solution.py:277
  157.6 3.8 %all-to-all-start.1 = ((bf16[4,128,2048]{2,1,0:T(8,128)(2,1)}), bf16[4,128,2048]{2,1,0:T(8,128)(2,1)S(1)}, u32[]{:S(2)}, u32[]{:S(2)}) async-start(bf16[4,128,2048]{2,1,0:T(8,128)(2,1)} %bitcast.124), calls=%async_computation.1 | async-start | bytes 4194304 | tf_op jit(solution)/shard_map/all_to_all | solution.py:39
  170.7 5.3 %fusion.21 = bf16[512,1280]{1,0:T(8,128)(2,1)} fusion(bf16[512,1280]{1,0:T(8,128)(2,1)S(1)} %copy-done.10, bf16[4,1280,1280]{2,1,0:T(8,128)(2,1)} %bitcast.119, s32[]{:T(128)S(6)} %select_n.220, bf16[512,1280]{1,0:T(8,128)(2,1)} %collective-permute-done.19), kind=kOutput, calls=%fused_computation.25 | convolution fusion | flops 1679687680 | bytes 7208964 | tf_op jit(solution)/shard_map/dot_general | solution.py:51
  176.0 4.9 %fusion.15 = bf16[512,1280]{1,0:T(8,128)(2,1)} fusion(bf16[512,1280]{1,0:T(8,128)(2,1)S(1)} %copy-done.10, bf16[4,1280,1280]{2,1,0:T(8,128)(2,1)} %bitcast.120, s32[]{:T(128)S(6)} %select_n.221), kind=kOutput, calls=%fused_computation.23 | convolution fusion | flops 1678376960 | bytes 5898244 | tf_op jit(solution)/shard_map/dot_general | solution.py:51
  197.0 8.1 %all-to-all-start.2 = ((bf16[128,2,2048]{2,1,0:T(2,128)(2,1)}), bf16[128,2,2048]{2,1,0:T(2,128)(2,1)S(1)}, u32[]{:S(2)}, u32[]{:S(2)}) async-start(bf16[128,2,2048]{2,1,0:T(2,128)(2,1)} %all_to_all.23), calls=%async_computation.2 | async-start | bytes 2097152 | tf_op jit(solution)/shard_map/all_to_all | solution.py:39
  217.1 3.2 %collective-permute-start.25 = (bf16[224,640]{1,0:T(8,128)(2,1)S(1)}, bf16[224,640]{1,0:T(8,128)(2,1)S(1)}, u32[]{:S(2)}, u32[]{:S(2)}) collective-permute-start(bf16[224,640]{1,0:T(8,128)(2,1)S(1)} %get-tuple-element.163), channel_id=1, source_target_pairs={{0,64},{32,96},{64,0},{96,32},{1,65},{33,97},{65,1},{97,33},{2,66}... | collective-permute-start | bytes 860168 | tf_op jit(solution)/shard_map/ppermute | solution.py:31
  222.4 7.9 %collective-permute-done.27 = bf16[224,640]{1,0:T(8,128)(2,1)S(1)} collective-permute-done((bf16[224,640]{1,0:T(8,128)(2,1)S(1)}, bf16[224,640]{1,0:T(8,128)(2,1)S(1)}, u32[]{:S(2)}, u32[]{:S(2)}) %collective-permute-start.27) | collective-permute-done | bytes 286752 | tf_op jit(solution)/shard_map/ppermute | solution.py:27
  230.3 3.4 %collective-permute-start.26 = (bf16[224,640]{1,0:T(8,128)(2,1)S(1)}, bf16[224,640]{1,0:T(8,128)(2,1)S(1)}, u32[]{:S(2)}, u32[]{:S(2)}) collective-permute-start(bf16[224,640]{1,0:T(8,128)(2,1)S(1)} %get-tuple-element.162), channel_id=1, source_target_pairs={{0,96},{4,36},{32,0},{36,68},{64,32},{68,100},{96,64},{100,4},{1,9... | collective-permute-start | bytes 860168 | tf_op jit(solution)/shard_map/ppermute | solution.py:27
  233.7 3.2 %fusion.34 = bf16[512,1280]{1,0:T(8,128)(2,1)} fusion(bf16[512,1280]{1,0:T(8,128)(2,1)S(1)} %copy-done, bf16[512,1280]{1,0:T(8,128)(2,1)} %collective-permute-done.30, bf16[512,1280]{1,0:T(8,128)(2,1)S(1)} %copy-done.1, f32[512]{0:T(512)S(1)} %broadcast_multiply_fusion, f32[512]{0:T(512)S(1)} %get-tuple-element.165, f32[1280]{0:T(1024)S(1)} %convert_element_type.249, ...), kind=kLoop, calls=%fused_computation.37 | loop fusion | flops 6553600 | bytes 5254144 | tf_op jit(solution)/shard_map/convert_element_type | solution.py:321
  (136 shorter events, 75.6 us)
Async XLA Ops:
  3.5 24.4 %collective-permute-start = (bf16[512,1280]{1,0:T(8,128)(2,1)S(1)}, bf16[512,1280]{1,0:T(8,128)(2,1)}, u32[]{:S(2)}, u32[]{:S(2)}) collective-permute-start(bf16[512,1280]{1,0:T(8,128)(2,1)S(1)} %fusion.31.part), channel_id=1, source_target_pairs={{0,1},{4,7},{1,2},{5,4},{2,3},{6,5},{3,0},{7,6},{8,9},{12,15},{9,1... | collective-permute-start | bytes 3932168 | tf_op jit(solution)/shard_map/ppermute | solution.py:27
  7.8 30.1 %all-to-all-start = ((bf16[128,2,2048]{2,1,0:T(2,128)(2,1)}), bf16[128,2,2048]{2,1,0:T(2,128)(2,1)}, u32[]{:S(2)}, u32[]{:S(2)}) async-start(bf16[128,2,2048]{2,1,0:T(2,128)(2,1)} %all_to_all.19), calls=%async_computation | async-start | bytes 2097152 | tf_op jit(solution)/shard_map/all_to_all | solution.py:39
  27.9 20.9 %collective-permute-start.1 = (bf16[512,1280]{1,0:T(8,128)(2,1)}, bf16[512,1280]{1,0:T(8,128)(2,1)}, u32[]{:S(2)}, u32[]{:S(2)}) collective-permute-start(bf16[512,1280]{1,0:T(8,128)(2,1)} %collective-permute-done.part), channel_id=1, source_target_pairs={{0,1},{4,7},{1,2},{5,4},{2,3},{6,5},{3,0},{7,6},{8,9},{12,15},{9,1... | collective-permute-start | bytes 3932168 | tf_op jit(solution)/shard_map/ppermute | solution.py:27
  48.8 30.1 %collective-permute-start.3 = (bf16[512,1280]{1,0:T(8,128)(2,1)}, bf16[512,1280]{1,0:T(8,128)(2,1)}, u32[]{:S(2)}, u32[]{:S(2)}) collective-permute-start(bf16[512,1280]{1,0:T(8,128)(2,1)} %collective-permute-done.1.part), channel_id=1, source_target_pairs={{0,1},{4,7},{1,2},{5,4},{2,3},{6,5},{3,0},{7,6},{8,9},{12,15},{9,1... | collective-permute-start | bytes 3932168 | tf_op jit(solution)/shard_map/ppermute | solution.py:27
  58.2 19.7 %collective-permute-start.4 = (bf16[128,2048]{1,0:T(8,128)(2,1)}, bf16[128,2048]{1,0:T(8,128)(2,1)}, u32[]{:S(2)}, u32[]{:S(2)}) collective-permute-start(bf16[128,2048]{1,0:T(8,128)(2,1)} %collective-permute-done.2), channel_id=1, source_target_pairs={{0,1},{4,7},{1,2},{5,4},{2,3},{6,5},{3,0},{7,6},{8,9},{12,15},{9,1... | collective-permute-start | bytes 1572872 | tf_op jit(solution)/shard_map/ppermute | solution.py:27
  88.4 35.3 %collective-permute-start.7 = (bf16[4,512,1280]{2,1,0:T(8,128)(2,1)}, bf16[4,512,1280]{2,1,0:T(8,128)(2,1)}, u32[]{:S(2)}, u32[]{:S(2)}) collective-permute-start(bf16[4,512,1280]{2,1,0:T(8,128)(2,1)} %bitcast_dynamic-update-slice_fusion.own_left), channel_id=1, source_target_pairs={{0,4},{4,0},{1,5},{5,1},{2,6},{6,2},{3,7},{7,3},{8,12},{12,8},{9,1... | collective-permute-start | bytes 15728648 | tf_op jit(solution)/shard_map/ppermute | solution.py:35
  99.1 16.1 %collective-permute-start.9 = (bf16[512,2048]{1,0:T(8,128)(2,1)S(1)}, bf16[512,2048]{1,0:T(8,128)(2,1)}, u32[]{:S(2)}, u32[]{:S(2)}) collective-permute-start(bf16[512,2048]{1,0:T(8,128)(2,1)S(1)} %bitcast.121), channel_id=1, source_target_pairs={{0,4},{4,0},{1,5},{5,1},{2,6},{6,2},{3,7},{7,3},{8,12},{12,8},{9,1... | collective-permute-start | bytes 6291464 | tf_op jit(solution)/shard_map/ppermute | solution.py:35
  112.7 28.0 %collective-permute-start.6 = (bf16[512,1280]{1,0:T(8,128)(2,1)}, bf16[512,1280]{1,0:T(8,128)(2,1)}, u32[]{:S(2)}, u32[]{:S(2)}) collective-permute-start(bf16[512,1280]{1,0:T(8,128)(2,1)} %fusion.12), channel_id=1, source_target_pairs={{0,1},{4,7},{1,2},{5,4},{2,3},{6,5},{3,0},{7,6},{8,9},{12,15},{9,1... | collective-permute-start | bytes 3932168 | tf_op jit(solution)/shard_map/ppermute | solution.py:27
  138.2 23.2 %collective-permute-start.11 = (bf16[4,160,640]{2,1,0:T(8,128)(2,1)}, bf16[4,160,640]{2,1,0:T(8,128)(2,1)}, u32[]{:S(2)}, u32[]{:S(2)}) collective-permute-start(bf16[4,160,640]{2,1,0:T(8,128)(2,1)} %get-tuple-element.115), channel_id=1, source_target_pairs={{0,8},{4,28},{8,16},{12,4},{16,24},{20,12},{24,0},{28,20},{1,9},{5... | collective-permute-start | bytes 2457608 | tf_op jit(solution)/shard_map/ppermute | solution.py:27
  139.7 21.6 %collective-permute-start.12 = (bf16[4,160,640]{2,1,0:T(8,128)(2,1)}, bf16[4,160,640]{2,1,0:T(8,128)(2,1)}, u32[]{:S(2)}, u32[]{:S(2)}) collective-permute-start(bf16[4,160,640]{2,1,0:T(8,128)(2,1)} %get-tuple-element.116), channel_id=1, source_target_pairs={{0,32},{4,100},{32,64},{36,4},{64,96},{68,36},{96,0},{100,68},{1,3... | collective-permute-start | bytes 2457608 | tf_op jit(solution)/shard_map/ppermute | solution.py:27
  146.1 24.6 %collective-permute-start.19 = (bf16[512,1280]{1,0:T(8,128)(2,1)}, bf16[512,1280]{1,0:T(8,128)(2,1)}, u32[]{:S(2)}, u32[]{:S(2)}) collective-permute-start(bf16[512,1280]{1,0:T(8,128)(2,1)} %fusion.18), channel_id=1, source_target_pairs={{0,1},{4,7},{1,2},{5,4},{2,3},{6,5},{3,0},{7,6},{8,9},{12,15},{9,1... | collective-permute-start | bytes 3932168 | tf_op jit(solution)/shard_map/ppermute | solution.py:27
  157.6 34.0 %all-to-all-start.1 = ((bf16[4,128,2048]{2,1,0:T(8,128)(2,1)}), bf16[4,128,2048]{2,1,0:T(8,128)(2,1)S(1)}, u32[]{:S(2)}, u32[]{:S(2)}) async-start(bf16[4,128,2048]{2,1,0:T(8,128)(2,1)} %bitcast.124), calls=%async_computation.1 | async-start | bytes 4194304 | tf_op jit(solution)/shard_map/all_to_all | solution.py:39
  169.9 16.4 %collective-permute-start.15 = (bf16[4,64,640]{2,1,0:T(8,128)(2,1)S(1)}, bf16[4,64,640]{2,1,0:T(8,128)(2,1)S(1)}, u32[]{:S(2)}, u32[]{:S(2)}) collective-permute-start(bf16[4,64,640]{2,1,0:T(8,128)(2,1)S(1)} %fusion.46), channel_id=1, source_target_pairs={{0,8},{4,28},{8,16},{12,4},{16,24},{20,12},{24,0},{28,20},{1,9},{5... | collective-permute-start | bytes 983048 | tf_op jit(solution)/shard_map/ppermute | solution.py:27
  170.0 16.3 %collective-permute-start.16 = (bf16[4,64,640]{2,1,0:T(8,128)(2,1)S(1)}, bf16[4,64,640]{2,1,0:T(8,128)(2,1)S(1)}, u32[]{:S(2)}, u32[]{:S(2)}) collective-permute-start(bf16[4,64,640]{2,1,0:T(8,128)(2,1)S(1)} %fusion.45), channel_id=1, source_target_pairs={{0,32},{4,100},{32,64},{36,4},{64,96},{68,36},{96,0},{100,68},{1,3... | collective-permute-start | bytes 983048 | tf_op jit(solution)/shard_map/ppermute | solution.py:27
  187.9 17.2 %collective-permute-start.20 = (bf16[4,160,640]{2,1,0:T(8,128)(2,1)}, bf16[4,160,640]{2,1,0:T(8,128)(2,1)}, u32[]{:S(2)}, u32[]{:S(2)}) collective-permute-start(bf16[4,160,640]{2,1,0:T(8,128)(2,1)} %fusion.39), channel_id=1, source_target_pairs={{0,8},{4,28},{8,16},{12,4},{16,24},{20,12},{24,0},{28,20},{1,9},{5... | collective-permute-start | bytes 2457608 | tf_op jit(solution)/shard_map/ppermute | solution.py:27
  188.5 16.7 %collective-permute-start.21 = (bf16[4,160,640]{2,1,0:T(8,128)(2,1)}, bf16[4,160,640]{2,1,0:T(8,128)(2,1)}, u32[]{:S(2)}, u32[]{:S(2)}) collective-permute-start(bf16[4,160,640]{2,1,0:T(8,128)(2,1)} %fusion.38), channel_id=1, source_target_pairs={{0,32},{4,100},{32,64},{36,4},{64,96},{68,36},{96,0},{100,68},{1,3... | collective-permute-start | bytes 2457608 | tf_op jit(solution)/shard_map/ppermute | solution.py:27
  189.5 27.7 %collective-permute-start.30 = (bf16[512,1280]{1,0:T(8,128)(2,1)}, bf16[512,1280]{1,0:T(8,128)(2,1)}, u32[]{:S(2)}, u32[]{:S(2)}) collective-permute-start(bf16[512,1280]{1,0:T(8,128)(2,1)} %fusion.21), channel_id=1, source_target_pairs={{0,1},{4,7},{1,2},{5,4},{2,3},{6,5},{3,0},{7,6},{8,9},{12,15},{9,1... | collective-permute-start | bytes 3932168 | tf_op jit(solution)/shard_map/ppermute | solution.py:27
  191.5 16.9 %collective-permute-start.22 = (bf16[4,64,640]{2,1,0:T(8,128)(2,1)}, bf16[4,64,640]{2,1,0:T(8,128)(2,1)}, u32[]{:S(2)}, u32[]{:S(2)}) collective-permute-start(bf16[4,64,640]{2,1,0:T(8,128)(2,1)} %fusion.47), channel_id=1, source_target_pairs={{0,8},{4,28},{8,16},{12,4},{16,24},{20,12},{24,0},{28,20},{1,9},{5... | collective-permute-start | bytes 983048 | tf_op jit(solution)/shard_map/ppermute | solution.py:27
  197.0 41.3 %all-to-all-start.2 = ((bf16[128,2,2048]{2,1,0:T(2,128)(2,1)}), bf16[128,2,2048]{2,1,0:T(2,128)(2,1)S(1)}, u32[]{:S(2)}, u32[]{:S(2)}) async-start(bf16[128,2,2048]{2,1,0:T(2,128)(2,1)} %all_to_all.23), calls=%async_computation.2 | async-start | bytes 2097152 | tf_op jit(solution)/shard_map/all_to_all | solution.py:39
  210.2 20.1 %collective-permute-start.27 = (bf16[224,640]{1,0:T(8,128)(2,1)S(1)}, bf16[224,640]{1,0:T(8,128)(2,1)S(1)}, u32[]{:S(2)}, u32[]{:S(2)}) collective-permute-start(bf16[224,640]{1,0:T(8,128)(2,1)S(1)} %get-tuple-element.161), channel_id=1, source_target_pairs={{0,8},{4,28},{8,16},{12,4},{16,24},{20,12},{24,0},{28,20},{1,9},{5... | collective-permute-start | bytes 860168 | tf_op jit(solution)/shard_map/ppermute | solution.py:27
  211.2 25.7 %collective-permute-start.28 = (bf16[224,640]{1,0:T(8,128)(2,1)S(1)}, bf16[224,640]{1,0:T(8,128)(2,1)S(1)}, u32[]{:S(2)}, u32[]{:S(2)}) collective-permute-start(bf16[224,640]{1,0:T(8,128)(2,1)S(1)} %get-tuple-element.160), channel_id=1, source_target_pairs={{0,16},{8,24},{16,0},{24,8},{1,17},{9,25},{17,1},{25,9},{2,18},{10... | collective-permute-start | bytes 860168 | tf_op jit(solution)/shard_map/ppermute | solution.py:31
  213.9 23.0 %collective-permute-start.29 = (bf16[224,640]{1,0:T(8,128)(2,1)S(1)}, bf16[224,640]{1,0:T(8,128)(2,1)S(1)}, u32[]{:S(2)}, u32[]{:S(2)}) collective-permute-start(bf16[224,640]{1,0:T(8,128)(2,1)S(1)} %get-tuple-element.159), channel_id=1, source_target_pairs={{0,24},{4,12},{8,0},{12,20},{16,8},{20,28},{24,16},{28,4},{1,25},{... | collective-permute-start | bytes 860168 | tf_op jit(solution)/shard_map/ppermute | solution.py:27
  215.5 21.5 %collective-permute-start.24 = (bf16[224,640]{1,0:T(8,128)(2,1)S(1)}, bf16[224,640]{1,0:T(8,128)(2,1)S(1)}, u32[]{:S(2)}, u32[]{:S(2)}) collective-permute-start(bf16[224,640]{1,0:T(8,128)(2,1)S(1)} %get-tuple-element.164), channel_id=1, source_target_pairs={{0,32},{4,100},{32,64},{36,4},{64,96},{68,36},{96,0},{100,68},{1,3... | collective-permute-start | bytes 860168 | tf_op jit(solution)/shard_map/ppermute | solution.py:27
  217.1 19.8 %collective-permute-start.25 = (bf16[224,640]{1,0:T(8,128)(2,1)S(1)}, bf16[224,640]{1,0:T(8,128)(2,1)S(1)}, u32[]{:S(2)}, u32[]{:S(2)}) collective-permute-start(bf16[224,640]{1,0:T(8,128)(2,1)S(1)} %get-tuple-element.163), channel_id=1, source_target_pairs={{0,64},{32,96},{64,0},{96,32},{1,65},{33,97},{65,1},{97,33},{2,66}... | collective-permute-start | bytes 860168 | tf_op jit(solution)/shard_map/ppermute | solution.py:31
  (27 other events, 237.2 us)
